TPU v7x, 32 devices: a whole 2x2x4 slice. The times are simulated.
32 devices in a mesh: dp: 8 (over y, x, core), tensor: 4 (over z).
Axes of the slice: x: 2, y: 2, z: 4, core: 2. Of those that a mesh axis runs over, the one named last changes fastest.
Arguments:
- tokens_in: bfloat16 [8192, 1536], P('dp'), may hold values from -6 to 6
- doc_ids: int32 [8192], replicated, may hold values from 0 to 3, never falling along the last dimension, each value on 1 to 4096 neighbouring positions
- out_grad: bfloat16 [8192, 1536], P('dp'), may hold values from -6 to 6
- norm_gains: bfloat16 [2, 1536], replicated, may hold values from 0.5 to 1.5
- conv_taps: bfloat16 [3, 1536], P(None, 'tensor'), may hold values from -3.5 to 3.5
- stream_weight: bfloat16 [3, 1536, 1536], P(None, None, 'tensor'), may hold values from -0.15625 to 0.15625
- mixer_weight: bfloat16 [1536, 1536], P('tensor'), may hold values from -0.15625 to 0.15625
- hidden_weight: bfloat16 [2, 1536, 6912], P(None, None, 'tensor'), may hold values from -0.15625 to 0.15625
- down_weight: bfloat16 [6912, 1536], P('tensor'), may hold values from -0.078125 to 0.078125
- gains_first: float32 [2, 1536], replicated, may hold values from -0.0009336855 to 0.0009336855
- gains_second: float32 [2, 1536], replicated, may hold values from 7.2647386e-09 to 7.264739e-08
- taps_first: float32 [3, 1536], P(None, 'tensor'), may hold values from -0.0009336855 to 0.0009336855
- taps_second: float32 [3, 1536], P(None, 'tensor'), may hold values from 7.2647386e-09 to 7.264739e-08
- stream_first: float32 [3, 1536, 1536], P(None, 'dp', 'tensor'), may hold values from -0.0009336855 to 0.0009336855
- stream_second: float32 [3, 1536, 1536], P(None, 'dp', 'tensor'), may hold values from 7.2647386e-09 to 7.264739e-08
- mixer_first: float32 [1536, 1536], P('tensor', 'dp'), may hold values from -0.0009336855 to 0.0009336855
- mixer_second: float32 [1536, 1536], P('tensor', 'dp'), may hold values from 7.2647386e-09 to 7.264739e-08
- hidden_first: float32 [2, 1536, 6912], P(None, 'dp', 'tensor'), may hold values from -0.0009336855 to 0.0009336855
- hidden_second: float32 [2, 1536, 6912], P(None, 'dp', 'tensor'), may hold values from 7.2647386e-09 to 7.264739e-08
- down_first: float32 [6912, 1536], P('tensor', 'dp'), may hold values from -0.0009336855 to 0.0009336855
- down_second: float32 [6912, 1536], P('tensor', 'dp'), may hold values from 7.2647386e-09 to 7.264739e-08
Outputs:
- block_out: bfloat16 [8192, 1536], P('dp')
- input_grad: float32 [8192, 1536], P('dp')
- grad_norm: float32 [], replicated
- gains_grad: float32 [2, 1536], replicated
- gains_first_next: float32 [2, 1536], replicated
- gains_second_next: float32 [2, 1536], replicated
- gains_step: float32 [2, 1536], replicated
- taps_grad: float32 [3, 1536], P(None, 'tensor')
- taps_first_next: float32 [3, 1536], P(None, 'tensor')
- taps_second_next: float32 [3, 1536], P(None, 'tensor')
- taps_step: float32 [3, 1536], P(None, 'tensor')
- stream_grad: float32 [3, 1536, 1536], P(None, 'dp', 'tensor')
- stream_first_next: float32 [3, 1536, 1536], P(None, 'dp', 'tensor')
- stream_second_next: float32 [3, 1536, 1536], P(None, 'dp', 'tensor')
- stream_step: float32 [3, 1536, 1536], P(None, 'dp', 'tensor')
- mixer_grad: float32 [1536, 1536], P('tensor', 'dp')
- mixer_first_next: float32 [1536, 1536], P('tensor', 'dp')
- mixer_second_next: float32 [1536, 1536], P('tensor', 'dp')
- mixer_step: float32 [1536, 1536], P('tensor', 'dp')
- hidden_grad: float32 [2, 1536, 6912], P(None, 'dp', 'tensor')
- hidden_first_next: float32 [2, 1536, 6912], P(None, 'dp', 'tensor')
- hidden_second_next: float32 [2, 1536, 6912], P(None, 'dp', 'tensor')
- hidden_step: float32 [2, 1536, 6912], P(None, 'dp', 'tensor')
- down_grad: float32 [6912, 1536], P('tensor', 'dp')
- down_first_next: float32 [6912, 1536], P('tensor', 'dp')
- down_second_next: float32 [6912, 1536], P('tensor', 'dp')
- down_step: float32 [6912, 1536], P('tensor', 'dp')
Inputs may be any that keep to these rules, and one draw needn't show every extreme that they name: `doc_ids`: document ids never fall along the tokens; each document has 1 to 4096 tokens, and one has exactly 4096.
All inputs are finite; a program needn't handle non-finite values.
Results may differ from a plain program's by a relative error of at most 0.01.
The roundings to bfloat16 on the way count: a program that leaves them out, or rounds other values in their place, can miss the bound.
Values may be sent and summed in bfloat16 or wider, within the bound.
A program may use at most 256 MiB of HBM per device.

v0:
```python
import jax
import jax.numpy as jnp
from jax import lax
from jax.sharding import PartitionSpec as P

EPS_NORM = 1e-05
LEARN_RATE = 0.02
BETA_FIRST = 0.5
BETA_SECOND = 0.5
CORRECTION = 1.0 - 0.5**3
ADAM_EPS = 1e-08
DECAY_RATE = 0.1
CLIP_NORM = 1.0


def shifted(value, axis, steps):
    count = lax.axis_size(axis)
    leading, last = (max(0, -steps), min(count, count - steps))
    return lax.ppermute(value, axis, [(source, source + steps) for source in range(leading, last)])


def rms_scale(values):
    return lax.rsqrt(jnp.mean(values * values, axis=-1, keepdims=True) + EPS_NORM)


def norm_back(grad_normed, normal, inverse, gain_row):
    scaled = grad_normed * gain_row
    return inverse * (scaled - normal * jnp.mean(scaled * normal, axis=-1, keepdims=True))


def adam_step(master, gradient, first_moment, second_moment, factor, decay):
    clipped = gradient * factor
    first_next = BETA_FIRST * first_moment + (1.0 - BETA_FIRST) * clipped
    second_next = BETA_SECOND * second_moment + (1.0 - BETA_SECOND) * clipped * clipped
    change = -LEARN_RATE * (
        first_next / CORRECTION / (jnp.sqrt(second_next / CORRECTION) + ADAM_EPS) + decay * master
    )
    return (first_next, second_next, change)


def own_share(weight, share):
    offset_row = lax.axis_index("dp") * share
    return lax.dynamic_slice_in_dim(weight, offset_row, share, 1).astype(jnp.float32)


def contract_rows(left, right):
    return lax.dot_general(
        left, right, (((0,), (0,)), ((), ())), preferred_element_type=jnp.float32
    )


def contract_cols(left, right):
    return lax.dot_general(
        left, right, (((1,), (1,)), ((), ())), preferred_element_type=jnp.float32
    )


def squares(values):
    return jnp.sum(values * values)


def body(
    tokens_in,
    doc_ids,
    out_grad,
    norm_gains,
    conv_taps,
    stream_weight,
    mixer_weight,
    hidden_weight,
    down_weight,
    gains_first,
    gains_second,
    taps_first,
    taps_second,
    stream_first,
    stream_second,
    mixer_first,
    mixer_second,
    hidden_first,
    hidden_second,
    down_first,
    down_second,
):
    tok_rows = tokens_in.shape[0]
    kernel = conv_taps.shape[0]
    reach = kernel - 1
    first_row = lax.axis_index("dp") * tok_rows
    filler = jnp.full((reach,), -1, jnp.int32)
    padded_ids = jnp.concatenate([filler, doc_ids, filler])
    window = lax.dynamic_slice_in_dim(padded_ids, first_row, tok_rows + 2 * reach)
    current = window[reach : reach + tok_rows]
    back_valid = [
        (window[reach - offset : reach - offset + tok_rows] == current).astype(jnp.float32)[:, None]
        for offset in range(kernel)
    ]
    ahead_valid = [
        (window[reach + offset : reach + offset + tok_rows] == current).astype(jnp.float32)[:, None]
        for offset in range(kernel)
    ]
    tokens = tokens_in.astype(jnp.float32)
    gain_pair = norm_gains.astype(jnp.float32)
    tap_values = conv_taps.astype(jnp.float32)
    scale_one = rms_scale(tokens)
    normal_one = tokens * scale_one
    normed_one = (normal_one * gain_pair[0]).astype(jnp.bfloat16)
    streams = jnp.einsum(
        "td,sdc->stc", normed_one, stream_weight, preferred_element_type=jnp.float32
    )
    product = (streams[0] * streams[2]).astype(jnp.bfloat16)
    edge_rows = shifted(product[tok_rows - reach :], "dp", 1)
    extended = jnp.concatenate([edge_rows, product], 0).astype(jnp.float32)
    conv_out = tap_values[0] * extended[reach : reach + tok_rows] * back_valid[0]
    for offset in range(1, kernel):
        conv_out = (
            conv_out
            + tap_values[offset]
            * extended[reach - offset : reach - offset + tok_rows]
            * back_valid[offset]
        )
    gated_rows = (streams[1] * conv_out).astype(jnp.bfloat16)
    branch_part = jnp.dot(gated_rows, mixer_weight, preferred_element_type=jnp.float32)
    branch = lax.psum(branch_part, "tensor")
    middle = tokens + branch
    scale_two = rms_scale(middle)
    normal_two = middle * scale_two
    normed_two = (normal_two * gain_pair[1]).astype(jnp.bfloat16)
    hidden = jnp.einsum(
        "td,sdf->stf", normed_two, hidden_weight, preferred_element_type=jnp.float32
    )
    sigmoid_gate = jax.nn.sigmoid(hidden[0])
    silu_gate = hidden[0] * sigmoid_gate
    active = (silu_gate * hidden[1]).astype(jnp.bfloat16)
    feed_part = jnp.dot(active, down_weight, preferred_element_type=jnp.float32)
    feed_out = lax.psum(feed_part.astype(jnp.bfloat16), "tensor").astype(jnp.float32)
    block_out = (middle + feed_out).astype(jnp.bfloat16)
    upstream = out_grad.astype(jnp.float32)
    down_part = contract_rows(active, out_grad)
    grad_active = contract_cols(out_grad, down_weight)
    grad_gate = grad_active * hidden[1] * sigmoid_gate * (1.0 + hidden[0] * (1.0 - sigmoid_gate))
    grad_up = grad_active * silu_gate
    grad_hidden = jnp.stack([grad_gate, grad_up]).astype(jnp.bfloat16)
    hidden_part = jnp.einsum(
        "td,stf->sdf", normed_two, grad_hidden, preferred_element_type=jnp.float32
    )
    normed_two_part = jnp.einsum(
        "stf,sdf->td", grad_hidden, hidden_weight, preferred_element_type=jnp.float32
    )
    grad_normed_two = lax.psum(normed_two_part, "tensor")
    gain_two_part = jnp.sum(grad_normed_two * normal_two, axis=0)
    grad_middle = upstream + norm_back(grad_normed_two, normal_two, scale_two, gain_pair[1])
    grad_branch = grad_middle.astype(jnp.bfloat16)
    mixer_part = contract_rows(gated_rows, grad_branch)
    grad_gated = contract_cols(grad_branch, mixer_weight)
    grad_c = grad_gated * conv_out
    grad_conv = (grad_gated * streams[1]).astype(jnp.bfloat16)
    ahead_rows = shifted(grad_conv[:reach], "dp", -1)
    trailing = jnp.concatenate([grad_conv, ahead_rows], 0).astype(jnp.float32)
    grad_conv_wide = trailing[:tok_rows]
    taps_part = jnp.stack(
        [
            jnp.sum(
                grad_conv_wide
                * extended[reach - offset : reach - offset + tok_rows]
                * back_valid[offset],
                axis=0,
            )
            for offset in range(kernel)
        ]
    )
    grad_product = tap_values[0] * grad_conv_wide * ahead_valid[0]
    for offset in range(1, kernel):
        grad_product = (
            grad_product
            + tap_values[offset] * trailing[offset : offset + tok_rows] * ahead_valid[offset]
        )
    grad_streams = jnp.stack([grad_product * streams[2], grad_c, grad_product * streams[0]]).astype(
        jnp.bfloat16
    )
    stream_part = jnp.einsum(
        "td,stc->sdc", normed_one, grad_streams, preferred_element_type=jnp.float32
    )
    normed_one_part = jnp.einsum(
        "stc,sdc->td", grad_streams, stream_weight, preferred_element_type=jnp.float32
    )
    grad_normed_one = lax.psum(normed_one_part, "tensor")
    gain_one_part = jnp.sum(grad_normed_one * normal_one, axis=0)
    input_grad = grad_middle + norm_back(grad_normed_one, normal_one, scale_one, gain_pair[0])
    gain_stack = jnp.stack([gain_one_part, gain_two_part])
    gains_grad, taps_grad = lax.psum((gain_stack, taps_part), "dp")
    stream_total, mixer_total, hidden_total, down_total = (
        lax.psum_scatter(stream_part, "dp", scatter_dimension=1, tiled=True),
        lax.psum_scatter(mixer_part, "dp", scatter_dimension=1, tiled=True),
        lax.psum_scatter(hidden_part, "dp", scatter_dimension=1, tiled=True),
        lax.psum_scatter(down_part, "dp", scatter_dimension=1, tiled=True),
    )
    first_dp = (lax.axis_index("dp") == 0).astype(jnp.float32)
    first_tensor = (lax.axis_index("tensor") == 0).astype(jnp.float32)
    local_square = (
        squares(stream_total) + squares(mixer_total) + squares(hidden_total) + squares(down_total)
    )
    local_square = local_square + first_dp * (
        squares(taps_grad) + first_tensor * squares(gains_grad)
    )
    square_total = lax.psum(local_square, ("dp", "tensor"))
    grad_norm = jnp.sqrt(square_total)
    factor = jnp.minimum(1.0, CLIP_NORM / (grad_norm + 1e-06))
    gains_out = adam_step(gain_pair, gains_grad, gains_first, gains_second, factor, 0.0)
    taps_out = adam_step(tap_values, taps_grad, taps_first, taps_second, factor, DECAY_RATE)
    stream_out = adam_step(
        own_share(stream_weight, stream_total.shape[1]),
        stream_total,
        stream_first,
        stream_second,
        factor,
        DECAY_RATE,
    )
    mixer_out = adam_step(
        own_share(mixer_weight, mixer_total.shape[1]),
        mixer_total,
        mixer_first,
        mixer_second,
        factor,
        DECAY_RATE,
    )
    hidden_out = adam_step(
        own_share(hidden_weight, hidden_total.shape[1]),
        hidden_total,
        hidden_first,
        hidden_second,
        factor,
        DECAY_RATE,
    )
    down_out = adam_step(
        own_share(down_weight, down_total.shape[1]),
        down_total,
        down_first,
        down_second,
        factor,
        DECAY_RATE,
    )
    return (
        block_out,
        input_grad,
        grad_norm,
        gains_grad,
        gains_out[0],
        gains_out[1],
        gains_out[2],
        taps_grad,
        taps_out[0],
        taps_out[1],
        taps_out[2],
        stream_total,
        stream_out[0],
        stream_out[1],
        stream_out[2],
        mixer_total,
        mixer_out[0],
        mixer_out[1],
        mixer_out[2],
        hidden_total,
        hidden_out[0],
        hidden_out[1],
        hidden_out[2],
        down_total,
        down_out[0],
        down_out[1],
        down_out[2],
    )


def solution(mesh):
    return jax.shard_map(
        body,
        mesh=mesh,
        in_specs=(
            P("dp", None),
            P(),
            P("dp", None),
            P(),
            P(None, "tensor"),
            P(None, None, "tensor"),
            P("tensor", None),
            P(None, None, "tensor"),
            P("tensor", None),
            P(),
            P(),
            P(None, "tensor"),
            P(None, "tensor"),
            P(None, "dp", "tensor"),
            P(None, "dp", "tensor"),
            P("tensor", "dp"),
            P("tensor", "dp"),
            P(None, "dp", "tensor"),
            P(None, "dp", "tensor"),
            P("tensor", "dp"),
            P("tensor", "dp"),
        ),
        out_specs=(
            P("dp", None),
            P("dp", None),
            P(),
            P(),
            P(),
            P(),
            P(),
            P(None, "tensor"),
            P(None, "tensor"),
            P(None, "tensor"),
            P(None, "tensor"),
            P(None, "dp", "tensor"),
            P(None, "dp", "tensor"),
            P(None, "dp", "tensor"),
            P(None, "dp", "tensor"),
            P("tensor", "dp"),
            P("tensor", "dp"),
            P("tensor", "dp"),
            P("tensor", "dp"),
            P(None, "dp", "tensor"),
            P(None, "dp", "tensor"),
            P(None, "dp", "tensor"),
            P(None, "dp", "tensor"),
            P("tensor", "dp"),
            P("tensor", "dp"),
            P("tensor", "dp"),
            P("tensor", "dp"),
        ),
        check_vma=False,
    )
```

profile of v0, /device:TPU:0, one launch (start us, length us, event | category | flops | bytes accessed | tf_op | source)
XLA Modules:
  0.0 1472.9 jit_solution(3615150835446457697)
XLA Ops:
  8.2 3.0 fusion.11
  11.3 4.3 convolution_bitcast_fusion.4
  15.6 2.2 copy-done.6
  19.4 3.0 collective-permute-start
  23.0 1.5 concatenate.10
  24.4 1.6 fusion.41
  27.3 3.9 multiply_convert_fusion.8
  32.0 4.5 fusion.54
  36.8 224.8 %all-reduce.8.cloned.1.call-done = f32[1024,1536]{1,0:T(8,128)} async-done(((f32[1024,1536]{1,0:T(8,128)}), f32[1024,1536]{1,0:T(8,128)}) %all-reduce.8.cloned.1.call-update) | async-done | bytes 6291472 | tf_op jit(solution)/shard_map/psum | solution.py:123
  261.6 4.6 multiply_reduce_fusion.2
  266.2 2.7 copy-done.2
  268.9 17.3 %convolution_bitcast_fusion.1 = f32[2,1024,1728]{1,2,0:T(8,128)} fusion(bf16[2,1536,1728]{1,2,0:T(8,128)(2,1)} %param.28, f32[1024,1536]{1,0:T(8,128)S(1)} %get-tuple-element.146, f32[1536]{0:T(1024)S(1)} %get-tuple-element.115, f32[1024]{0:T(1024)S(1)} %add_rsqrt_fusion), kind=kOutput, calls=%fused_computation.16 | convolution fusion | flops 10876354560 | bytes 31074304 | tf_op jit(solution)/shard_map/td,sdf->stf/dot_general | solution.py:128
  286.2 16.0 %fusion.15 = (bf16[1,1024,1728]{1,2,0:T(8,128)(2,1)}, bf16[1,1024,1728]{1,2,0:T(8,128)(2,1)}, bf16[1024,1728]{0,1:T(8,128)(2,1)}) fusion(f32[2,1024,1728]{1,2,0:T(8,128)} %convolution_bitcast_fusion.1, bf16[1024,1536]{1,0:T(8,128)(2,1)S(1)} %copy-done.13, bf16[1728,1536]{1,0:T(8,128)(2,1)} %param.29), kind=kOutput, calls=%fused_computation.38 | convolution fusion | flops 5462360064 | bytes 33226752 | tf_op jit(solution)/shard_map/dot_general | solution.py:53
  302.2 16.0 %fusion.13 = f32[1024,1536]{1,0:T(8,128)} fusion(bf16[2,1536,1728]{1,2,0:T(8,128)(2,1)S(1)} %bitcast.95, bf16[1,1024,1728]{1,2,0:T(8,128)(2,1)} %get-tuple-element.150, bf16[1,1024,1728]{1,2,0:T(8,128)(2,1)} %get-tuple-element.149), kind=kOutput, calls=%fused_computation.33 | convolution fusion | flops 10875174912 | bytes 23986176 | tf_op jit(solution)/shard_map/stf,sdf->td/dot_general | solution.py:146
  318.3 10.2 convolution_convert_fusion
  328.5 211.6 %all-reduce.12.cloned.1.call-done = f32[1024,1536]{1,0:T(8,128)} async-done(((f32[1024,1536]{1,0:T(8,128)}), f32[1024,1536]{1,0:T(8,128)}) %all-reduce.12.cloned.1.call-update) | async-done | bytes 6291472 | tf_op jit(solution)/shard_map/psum | solution.py:149
  540.1 6.1 multiply_reduce_fusion
  546.8 116.2 %all-reduce.10.cloned.1.call-done = bf16[1024,1536]{1,0:T(8,128)(2,1)} async-done(((bf16[1024,1536]{1,0:T(8,128)(2,1)}), bf16[1024,1536]{1,0:T(8,128)(2,1)}) %all-reduce.10.cloned.1.call-update) | async-done | bytes 3145744 | tf_op jit(solution)/shard_map/psum | solution.py:135
  663.0 9.4 multiply_add_fusion
  672.4 2.7 copy-done.1
  675.1 3.2 fusion.25
  678.6 19.5 %convolution_bitcast_fusion = f32[2,1536,1728]{1,2,0:T(8,128)} fusion(bf16[1,1024,1728]{1,2,0:T(8,128)(2,1)} %get-tuple-element.150, bf16[1,1024,1728]{1,2,0:T(8,128)(2,1)} %get-tuple-element.149, f32[1024,1536]{1,0:T(8,128)} %copy-done.2, f32[1536]{0:T(1024)S(1)} %get-tuple-element.115, f32[1024]{0:T(1024)S(1)} %add_rsqrt_fusion), kind=kOutput, calls=%fused_computation | convolution fusion | flops 10879893504 | bytes 34613248 | tf_op jit(solution)/shard_map/td,stf->sdf/dot_general | solution.py:143
  698.1 32.6 %copy.83 = f32[2,1536,1728]{2,0,1:T(2,128)} copy(f32[2,1536,1728]{1,2,0:T(8,128)} %convolution_bitcast_fusion) | data formatting | bytes 42467328 | tf_op jit(solution)/shard_map/td,stf->sdf/transpose | solution.py:143
  730.9 5.0 fusion.27
  736.0 1.9 fusion.32
  739.2 1.8 collective-permute-done.1
  741.1 3.3 multiply_reduce_fusion.6
  744.4 1.9 fusion.33
  747.3 6.3 convolution_bitcast_fusion.3
  753.6 11.2 fusion.55
  765.5 10.0 convolution_bitcast_fusion.2
  775.4 10.9 copy.97
  786.3 7.3 copy.104
  794.4 2.1 copy.100
  796.5 2.5 copy.85
  799.0 2.6 copy.84
  801.6 1.8 constant_dynamic-slice_fusion.2
  803.4 1.7 copy.101
  805.1 4.0 constant_dynamic-slice_fusion.1
  809.0 2.6 copy.102
  811.7 2.6 constant_dynamic-slice_fusion
  814.3 2.3 copy.103
  821.8 1.6 multiply_reduce_fusion.9
  823.4 179.7 %all-reduce.16.cloned.1.call-done = f32[2,1536,1728]{2,0,1:T(2,128)} async-done(((f32[2,1536,1728]{2,0,1:T(2,128)}), f32[2,1536,1728]{2,0,1:T(2,128)}) %all-reduce.16.cloned.1.call-update) | async-done | bytes 21233680
  1003.1 6.7 multiply_reduce_fusion.3
  1009.7 218.6 %all-reduce.14.cloned.1.call-done = f32[1024,1536]{1,0:T(8,128)} async-done(((f32[1024,1536]{1,0:T(8,128)}), f32[1024,1536]{1,0:T(8,128)}) %all-reduce.14.cloned.1.call-update) | async-done | bytes 6291472 | tf_op jit(solution)/shard_map/psum | solution.py:186
  1228.3 4.7 fusion.10
  1233.6 25.3 %all-reduce.1 = (f32[3,384]{1,0:T(4,128)}, f32[2,1536]{1,0:T(2,128)}) all-reduce(f32[3,384]{1,0:T(4,128)} %pad_maximum_fusion.9, f32[2,1536]{1,0:T(2,128)} %pad_maximum_fusion.8), channel_id=1, replica_groups=mesh['dp'=8,'tensor'=4] {'dp'}, use_global_device_ids=true, to_apply=%region_19.0 | all-reduce | flops 4224 | bytes 33792 | tf_op jit(solution)/shard_map/psum | solution.py:190
  1262.9 9.6 fusion.9
  1272.5 43.3 %reduce-scatter.8.cloned.1.call-done = f32[1728,192]{0,1:T(8,128)} async-done(((f32[1728,1536]{0,1:T(8,128)}), f32[1728,192]{0,1:T(8,128)}) %reduce-scatter.8.cloned.1.call-update) | async-done | bytes 1327120 | tf_op jit(solution)/shard_map/reduce_scatter | solution.py:195
  1315.8 2.3 multiply_reduce_fusion.7
  1318.1 66.8 %reduce-scatter.10.cloned.1.call-done = f32[192,1152]{1,0:T(8,128)} async-done(((f32[1536,1152]{1,0:T(8,128)}), f32[192,1152]{1,0:T(8,128)}) %reduce-scatter.10.cloned.1.call-update) | async-done | bytes 884752
  1384.9 2.3 reshape.87
  1387.2 2.4 copy.98
  1389.6 2.2 multiply_reduce_fusion.8
  1394.4 2.2 copy.91
  1396.6 39.2 %psum.55 = f32[]{:T(128)} all-reduce(f32[]{:T(128)S(6)} %add.202), channel_id=1, replica_groups=mesh['dp'=8,'tensor'=4] {'dp','tensor'}, use_global_device_ids=true, to_apply=%region_25.0 | all-reduce | flops 1 | bytes 8 | tf_op jit(solution)/shard_map/psum | solution.py:205
  1436.6 4.6 add_multiply_fusion.2
  1441.2 2.6 copy.92
  1443.8 2.5 copy.93
  1446.3 2.5 copy.94
  1448.8 1.4 add_multiply_fusion.4
  1451.6 8.9 add_multiply_fusion
  1461.7 2.8 add_multiply_fusion.1
  (132 shorter events, 20.8 us)
Async XLA Ops:
  7.2 4.0 copy-start
  7.2 254.4 %all-reduce.8.cloned.1.call-start = ((), (), s32[]{:S(2)}) async-start(), calls=%async_computation.3 | async-start | bytes 12582912 | tf_op jit(solution)/shard_map/psum | solution.py:123
  7.3 4.0 copy-start.5
  8.2 7.4 copy-start.24
  11.2 4.3 copy-start.29
  15.6 2.2 copy-start.6
  17.8 4.6 copy-start.38
  17.9 0.9 copy-start.12
  19.4 6.6 collective-permute-start
  23.0 8.2 copy-start.32
  26.0 5.2 copy-start.27
  27.3 3.9 copy-start.3
  27.3 4.8 copy-start.10
  31.2 0.9 copy-start.7
  36.6 503.5 %all-reduce.12.cloned.1.call-start = ((), (), s32[]{:S(2)}) async-start(), calls=%async_computation.5 | async-start | bytes 12582912 | tf_op jit(solution)/shard_map/psum | solution.py:149
  266.2 2.7 copy-start.2
  268.9 17.3 %copy-start.13 = (bf16[1024,1536]{1,0:T(8,128)(2,1)S(1)}, bf16[1024,1536]{1,0:T(8,128)(2,1)}, u32[]{:S(2)}) copy-start(bf16[1024,1536]{1,0:T(8,128)(2,1)} %param.23) | copy-start | bytes 9437188
  268.9 33.3 %slice-start = ((s8[10616832]{0:T(1024)(128)(4,1)}), s8[2228224]{0:T(1024)(128)(4,1)S(1)}, s32[]{:S(2)}) async-start(s8[10616832]{0:T(1024)(128)(4,1)} %bitcast.94), calls=%async_computation.11 | async-start | bytes 4456448
  268.9 33.3 %slice-start.1 = ((s8[10616832]{0:T(1024)(128)(4,1)}), s8[4194304]{0:T(1024)(128)(4,1)S(1)}, s32[]{:S(2)}) async-start(s8[10616832]{0:T(1024)(128)(4,1)} %bitcast.94), calls=%async_computation.12 | async-start | bytes 8388608
  286.2 16.0 %slice-start.2 = ((s8[10616832]{0:T(1024)(128)(4,1)}), s8[4194304]{0:T(1024)(128)(4,1)S(1)}, s32[]{:S(2)}) async-start(s8[10616832]{0:T(1024)(128)(4,1)} %bitcast.94), calls=%async_computation.13 | async-start | bytes 8388608
  318.2 344.8 %all-reduce.10.cloned.1.call-start = ((), (), s32[]{:S(2)}) async-start(), calls=%async_computation.4 | async-start | bytes 6291456 | tf_op jit(solution)/shard_map/psum | solution.py:135
  328.5 493.3 %reduce-scatter.6.cloned.1.call-start = ((), (), s32[]{:S(2)}) async-start(), calls=%async_computation.7 | async-start | bytes 2654208 | tf_op jit(solution)/shard_map/reduce_scatter | solution.py:193
  663.0 12.1 copy-start.8
  672.4 2.7 copy-start.1
  678.4 324.7 %all-reduce.16.cloned.1.call-start = ((), (), s32[]{:S(2)}) async-start(), calls=%async_computation.10 | async-start | bytes 44040192
  730.8 497.5 %all-reduce.14.cloned.1.call-start = ((), (), s32[]{:S(2)}) async-start(), calls=%async_computation.6 | async-start | bytes 12582912 | tf_op jit(solution)/shard_map/psum | solution.py:186
  730.8 5.0 copy-start.9
  735.9 5.2 copy-start.4
  735.9 5.2 copy-start.28
  735.9 5.2 copy-start.33
  735.9 5.2 copy-start.34
  735.9 5.2 copy-start.35
  735.9 5.2 copy-start.36
  735.9 5.2 copy-start.37
  737.9 8.5 copy-start.18
  737.9 3.1 collective-permute-start.1
  744.4 2.0 copy-start.20
  746.4 0.9 copy-start.19
  753.5 562.3 %reduce-scatter.8.cloned.1.call-start = ((), (), s32[]{:S(2)}) async-start(), calls=%async_computation.8 | async-start | bytes 12386304 | tf_op jit(solution)/shard_map/reduce_scatter | solution.py:195
  764.8 0.7 copy-start.25
  764.8 0.7 copy-start.30
  764.8 620.1 %reduce-scatter.10.cloned.1.call-start = ((), (), s32[]{:S(2)}) async-start(), calls=%async_computation.9 | async-start | bytes 7962624
  809.0 12.1 copy-start.40
  1228.3 4.7 copy-start.31
  1441.2 7.6 copy-start.26
  1441.2 9.0 copy-start.39
  1451.6 9.0 copy-start.17
  1451.6 9.0 copy-start.21
  1451.6 9.0 copy-start.22
  1451.6 9.0 copy-start.23
  1451.6 10.1 copy-start.11
  1451.6 10.1 copy-start.14
  1451.6 10.1 copy-start.15
  1451.6 10.0 copy-start.16
Sparse Core Ops, SparseCore 0:
  36.7 224.8 all-reduce.7
  318.3 221.7 all-reduce.11
  543.1 119.9 all-reduce.9
  678.5 41.3 reduce-scatter.5
  730.9 272.1 all-reduce.15
  1005.3 222.9 all-reduce.13
  1232.4 83.3 reduce-scatter.7
  1319.3 65.4 reduce-scatter.9
where the time goes:
time: 1480 us; the launch traced here: 1470 us
  waiting for transfers between devices  1060 us (72%)
  matrix products  123 us (8%)
  local copies, waits for them, and re-layouts  106 us (7%)
  other arithmetic  89.6 us (6%)
  blocking collectives  64.6 us (4%)
  between operations  21.5 us (1%)
    unnamed x10, waiting for transfers between devices  247 us
    psum x1, waiting for transfers between devices, body(): branch = lax.psum(branch_part, 'tensor')  225 us
    psum x1, waiting for transfers between devices, body(): grad_normed_one = lax.psum(normed_one_part, 'tensor')  219 us
    psum x1, waiting for transfers between devices, body(): grad_normed_two = lax.psum(normed_two_part, 'tensor')  212 us
    psum x1, waiting for transfers between devices, body(): lax.psum(feed_part.astype(jnp.bfloat16), 'tensor').astype(jnp.float32)  116 us
    unnamed x103, local copies, waits for them, and re-layouts  58.6 us
    reduce_scatter x1, waiting for transfers between devices, body(): lax.psum_scatter(down_part, 'dp', scatter_dimension=1, tiled=True)  43.3 us
    psum x1, blocking collectives, body(): square_total = lax.psum(local_square, ('dp', 'tensor'))  39.2 us
  transfers between devices with their start and end apart: 10, of which 8 were waited for; matrix products, arithmetic and copies ran while one was open for 13% of the time, Pallas kernels for 0%

commit v1 on v0

--- a/solution.py
+++ b/solution.py
@@ -120,7 +120,7 @@
         )
     gated_rows = (streams[1] * conv_out).astype(jnp.bfloat16)
     branch_part = jnp.dot(gated_rows, mixer_weight, preferred_element_type=jnp.float32)
-    branch = lax.psum(branch_part, "tensor")
+    branch = jnp.sum(lax.all_gather(branch_part, "tensor"), axis=0)
     middle = tokens + branch
     scale_two = rms_scale(middle)
     normal_two = middle * scale_two

time: 1480 us -> 1690 us (1.14)
  waiting for transfers between devices: 1060 us -> 1260 us
    all_gather x0 -> x1, waiting for transfers between devices: none -> 427 us  [body(): branch = jnp.sum(lax.all_gather(branch_part, 'tensor'), axis=0)]
    psum x1 -> x0, waiting for transfers between devices: 225 us -> none  [body(): branch = lax.psum(branch_part, 'tensor')]
  transfers between devices with their start and end apart: 10 -> 10, of which waited for: 8 -> 8; matrix products, arithmetic and copies ran while one was open for 13% -> 11% of each run, Pallas kernels for 0% -> 0%
where the time goes in v1:
time: 1690 us
  waiting for transfers between devices  1260 us (75%)
  matrix products  123 us (7%)
  local copies, waits for them, and re-layouts  106 us (6%)
  other arithmetic  103 us (6%)
  blocking collectives  64.6 us (4%)
  between operations  21.5 us (1%)
    all_gather x1, waiting for transfers between devices, body(): branch = jnp.sum(lax.all_gather(branch_part, 'tensor'), axis=0)  427 us
    unnamed x10, waiting for transfers between devices  247 us
    psum x1, waiting for transfers between devices, body(): grad_normed_one = lax.psum(normed_one_part, 'tensor')  219 us
    psum x1, waiting for transfers between devices, body(): grad_normed_two = lax.psum(normed_two_part, 'tensor')  211 us
    psum x1, waiting for transfers between devices, body(): lax.psum(feed_part.astype(jnp.bfloat16), 'tensor').astype(jnp.float32)  116 us
    unnamed x103, local copies, waits for them, and re-layouts  58.6 us
    reduce_scatter x1, waiting for transfers between devices, body(): lax.psum_scatter(down_part, 'dp', scatter_dimension=1, tiled=True)  43.3 us
    psum x1, blocking collectives, body(): square_total = lax.psum(local_square, ('dp', 'tensor'))  39.2 us
  transfers between devices with their start and end apart: 10, of which 8 were waited for; matrix products, arithmetic and copies ran while one was open for 11% of the time, Pallas kernels for 0%

profile of v1, /device:TPU:0, one launch (start us, length us, event | category | flops | bytes accessed | tf_op | source)
XLA Modules:
  0.0 1687.6 jit_solution(9208829163664806828)
XLA Ops:
  8.2 3.0 fusion.11
  11.3 4.3 convolution_bitcast_fusion.4
  15.6 2.2 copy-done.6
  19.4 3.0 collective-permute-start
  23.0 1.5 concatenate.10
  24.4 1.6 fusion.41
  27.3 3.9 multiply_convert_fusion.8
  32.0 4.5 fusion.54
  36.8 427.1 %all-gather.3.cloned.1.call-done = f32[4096,1536]{1,0:T(8,128)} async-done(((f32[1024,1536]{1,0:T(8,128)}), f32[4096,1536]{1,0:T(8,128)}) %all-gather.3.cloned.1.call-update) | async-done | bytes 25165840 | tf_op jit(solution)/shard_map/all_gather | solution.py:123
  463.9 13.2 reduce_sum.145
  477.1 4.6 multiply_reduce_fusion.2
  481.7 2.7 copy-done.2
  484.4 17.3 %convolution_bitcast_fusion.1 = f32[2,1024,1728]{1,2,0:T(8,128)} fusion(bf16[2,1536,1728]{1,2,0:T(8,128)(2,1)} %param.28, f32[1024,1536]{1,0:T(8,128)S(1)} %get-tuple-element.146, f32[1536]{0:T(1024)S(1)} %get-tuple-element.115, f32[1024]{0:T(1024)S(1)} %add_rsqrt_fusion), kind=kOutput, calls=%fused_computation.16 | convolution fusion | flops 10876354560 | bytes 31074304 | tf_op jit(solution)/shard_map/td,sdf->stf/dot_general | solution.py:128
  501.7 16.0 fusion.15
  517.7 16.0 fusion.13
  533.8 10.2 convolution_convert_fusion
  544.0 210.9 %all-reduce.9.cloned.1.call-done = f32[1024,1536]{1,0:T(8,128)} async-done(((f32[1024,1536]{1,0:T(8,128)}), f32[1024,1536]{1,0:T(8,128)}) %all-reduce.9.cloned.1.call-update) | async-done | bytes 6291472 | tf_op jit(solution)/shard_map/psum | solution.py:149
  754.9 6.1 multiply_reduce_fusion
  761.6 116.2 %all-reduce.7.cloned.1.call-done = bf16[1024,1536]{1,0:T(8,128)(2,1)} async-done(((bf16[1024,1536]{1,0:T(8,128)(2,1)}), bf16[1024,1536]{1,0:T(8,128)(2,1)}) %all-reduce.7.cloned.1.call-update) | async-done | bytes 3145744 | tf_op jit(solution)/shard_map/psum | solution.py:135
  877.8 9.4 multiply_add_fusion
  887.2 2.7 copy-done.1
  889.9 3.2 fusion.25
  893.4 19.5 %convolution_bitcast_fusion = f32[2,1536,1728]{1,2,0:T(8,128)} fusion(bf16[1,1024,1728]{1,2,0:T(8,128)(2,1)} %get-tuple-element.150, bf16[1,1024,1728]{1,2,0:T(8,128)(2,1)} %get-tuple-element.149, f32[1024,1536]{1,0:T(8,128)} %copy-done.2, f32[1536]{0:T(1024)S(1)} %get-tuple-element.115, f32[1024]{0:T(1024)S(1)} %add_rsqrt_fusion), kind=kOutput, calls=%fused_computation | convolution fusion | flops 10879893504 | bytes 34613248 | tf_op jit(solution)/shard_map/td,stf->sdf/dot_general | solution.py:143
  912.9 32.7 %copy.83 = f32[2,1536,1728]{2,0,1:T(2,128)} copy(f32[2,1536,1728]{1,2,0:T(8,128)} %convolution_bitcast_fusion) | data formatting | bytes 42467328 | tf_op jit(solution)/shard_map/td,stf->sdf/transpose | solution.py:143
  945.6 5.0 fusion.27
  950.8 1.9 fusion.32
  954.0 1.8 collective-permute-done.1
  955.9 3.3 multiply_reduce_fusion.6
  959.2 1.9 fusion.33
  962.1 6.3 convolution_bitcast_fusion.3
  968.4 11.2 fusion.55
  980.3 10.0 convolution_bitcast_fusion.2
  990.2 10.8 copy.97
  1001.1 7.3 copy.104
  1009.2 2.1 copy.100
  1011.3 2.5 copy.85
  1013.8 2.6 copy.84
  1016.4 1.8 constant_dynamic-slice_fusion.2
  1018.1 1.7 copy.101
  1019.9 4.0 constant_dynamic-slice_fusion.1
  1023.8 2.6 copy.102
  1026.4 2.6 constant_dynamic-slice_fusion
  1029.0 2.3 copy.103
  1036.6 1.6 multiply_reduce_fusion.9
  1038.2 179.7 %all-reduce.13.cloned.1.call-done = f32[2,1536,1728]{2,0,1:T(2,128)} async-done(((f32[2,1536,1728]{2,0,1:T(2,128)}), f32[2,1536,1728]{2,0,1:T(2,128)}) %all-reduce.13.cloned.1.call-update) | async-done | bytes 21233680
  1217.9 6.7 multiply_reduce_fusion.3
  1224.5 218.6 %all-reduce.11.cloned.1.call-done = f32[1024,1536]{1,0:T(8,128)} async-done(((f32[1024,1536]{1,0:T(8,128)}), f32[1024,1536]{1,0:T(8,128)}) %all-reduce.11.cloned.1.call-update) | async-done | bytes 6291472 | tf_op jit(solution)/shard_map/psum | solution.py:186
  1443.1 4.7 fusion.10
  1448.4 25.3 %all-reduce.1 = (f32[3,384]{1,0:T(4,128)}, f32[2,1536]{1,0:T(2,128)}) all-reduce(f32[3,384]{1,0:T(4,128)} %pad_maximum_fusion.9, f32[2,1536]{1,0:T(2,128)} %pad_maximum_fusion.8), channel_id=1, replica_groups=mesh['dp'=8,'tensor'=4] {'dp'}, use_global_device_ids=true, to_apply=%region_19.0 | all-reduce | flops 4224 | bytes 33792 | tf_op jit(solution)/shard_map/psum | solution.py:190
  1477.7 9.6 fusion.9
  1487.3 43.3 %reduce-scatter.8.cloned.1.call-done = f32[1728,192]{0,1:T(8,128)} async-done(((f32[1728,1536]{0,1:T(8,128)}), f32[1728,192]{0,1:T(8,128)}) %reduce-scatter.8.cloned.1.call-update) | async-done | bytes 1327120 | tf_op jit(solution)/shard_map/reduce_scatter | solution.py:195
  1530.6 2.3 multiply_reduce_fusion.7
  1532.9 66.8 %reduce-scatter.10.cloned.1.call-done = f32[192,1152]{1,0:T(8,128)} async-done(((f32[1536,1152]{1,0:T(8,128)}), f32[192,1152]{1,0:T(8,128)}) %reduce-scatter.10.cloned.1.call-update) | async-done | bytes 884752
  1599.7 2.3 reshape.88
  1602.0 2.4 copy.98
  1604.4 2.2 multiply_reduce_fusion.8
  1609.2 2.2 copy.91
  1611.4 39.2 %psum.47 = f32[]{:T(128)} all-reduce(f32[]{:T(128)S(6)} %add.200), channel_id=1, replica_groups=mesh['dp'=8,'tensor'=4] {'dp','tensor'}, use_global_device_ids=true, to_apply=%region_25.0 | all-reduce | flops 1 | bytes 8 | tf_op jit(solution)/shard_map/psum | solution.py:205
  1651.4 4.6 add_multiply_fusion.2
  1656.0 2.6 copy.92
  1658.5 2.5 copy.93
  1661.1 2.5 copy.94
  1666.4 8.9 add_multiply_fusion
  1676.5 2.8 add_multiply_fusion.1
  (133 shorter events, 22.2 us)
Async XLA Ops:
  7.2 4.0 copy-start
  7.2 456.7 %all-gather.3.cloned.1.call-start = ((), (), s32[]{:S(2)}) async-start(), calls=%async_computation.8 | async-start | bytes 31457280 | tf_op jit(solution)/shard_map/all_gather | solution.py:123
  7.3 4.0 copy-start.5
  8.2 7.4 copy-start.24
  11.2 4.3 copy-start.29
  15.6 2.2 copy-start.6
  17.8 4.6 copy-start.38
  17.9 0.9 copy-start.12
  19.4 6.6 collective-permute-start
  23.0 8.2 copy-start.32
  26.0 5.2 copy-start.27
  27.3 3.9 copy-start.3
  27.3 4.8 copy-start.10
  31.2 0.9 copy-start.7
  36.6 718.3 %all-reduce.9.cloned.1.call-start = ((), (), s32[]{:S(2)}) async-start(), calls=%async_computation.4 | async-start | bytes 12582912 | tf_op jit(solution)/shard_map/psum | solution.py:149
  481.7 2.7 copy-start.2
  484.4 17.3 %copy-start.13 = (bf16[1024,1536]{1,0:T(8,128)(2,1)S(1)}, bf16[1024,1536]{1,0:T(8,128)(2,1)}, u32[]{:S(2)}) copy-start(bf16[1024,1536]{1,0:T(8,128)(2,1)} %param.23) | copy-start | bytes 9437188
  484.4 33.3 %slice-start = ((s8[10616832]{0:T(1024)(128)(4,1)}), s8[2228224]{0:T(1024)(128)(4,1)S(1)}, s32[]{:S(2)}) async-start(s8[10616832]{0:T(1024)(128)(4,1)} %bitcast.96), calls=%async_computation.11 | async-start | bytes 4456448
  484.4 33.3 %slice-start.1 = ((s8[10616832]{0:T(1024)(128)(4,1)}), s8[4194304]{0:T(1024)(128)(4,1)S(1)}, s32[]{:S(2)}) async-start(s8[10616832]{0:T(1024)(128)(4,1)} %bitcast.96), calls=%async_computation.12 | async-start | bytes 8388608
  501.7 16.0 slice-start.2
  533.7 344.1 %all-reduce.7.cloned.1.call-start = ((), (), s32[]{:S(2)}) async-start(), calls=%async_computation.3 | async-start | bytes 6291456 | tf_op jit(solution)/shard_map/psum | solution.py:135
  544.0 492.6 %reduce-scatter.6.cloned.1.call-start = ((), (), s32[]{:S(2)}) async-start(), calls=%async_computation.6 | async-start | bytes 2654208 | tf_op jit(solution)/shard_map/reduce_scatter | solution.py:193
  877.8 12.1 copy-start.8
  887.2 2.7 copy-start.1
  893.2 324.7 %all-reduce.13.cloned.1.call-start = ((), (), s32[]{:S(2)}) async-start(), calls=%async_computation.10 | async-start | bytes 44040192
  945.6 497.5 %all-reduce.11.cloned.1.call-start = ((), (), s32[]{:S(2)}) async-start(), calls=%async_computation.5 | async-start | bytes 12582912 | tf_op jit(solution)/shard_map/psum | solution.py:186
  945.6 5.0 copy-start.9
  950.7 5.2 copy-start.4
  950.7 5.2 copy-start.28
  950.7 5.2 copy-start.33
  950.7 5.2 copy-start.34
  950.7 5.2 copy-start.35
  950.7 5.2 copy-start.36
  950.7 5.2 copy-start.37
  952.7 8.5 copy-start.18
  952.7 3.1 collective-permute-start.1
  959.2 2.0 copy-start.20
  961.2 0.9 copy-start.19
  968.3 562.3 %reduce-scatter.8.cloned.1.call-start = ((), (), s32[]{:S(2)}) async-start(), calls=%async_computation.7 | async-start | bytes 12386304 | tf_op jit(solution)/shard_map/reduce_scatter | solution.py:195
  979.6 0.7 copy-start.25
  979.6 0.7 copy-start.30
  979.6 620.1 %reduce-scatter.10.cloned.1.call-start = ((), (), s32[]{:S(2)}) async-start(), calls=%async_computation.9 | async-start | bytes 7962624
  1023.8 12.1 copy-start.40
  1443.1 4.7 copy-start.31
  1656.0 7.6 copy-start.26
  1656.0 9.0 copy-start.39
  1666.4 9.0 copy-start.17
  1666.4 9.0 copy-start.21
  1666.4 9.0 copy-start.22
  1666.4 9.0 copy-start.23
  1666.4 10.1 copy-start.11
  1666.4 10.1 copy-start.14
  1666.4 10.1 copy-start.15
  1666.4 10.0 copy-start.16
Sparse Core Ops, SparseCore 0:
  36.7 427.1 all-gather.2
  533.8 221.0 all-reduce.8
  757.8 119.9 all-reduce.6
  893.3 41.3 reduce-scatter.5
  945.7 272.1 all-reduce.12
  1220.1 222.9 all-reduce.10
  1447.2 83.3 reduce-scatter.7
  1534.1 65.4 reduce-scatter.9
